TPU v7x, 32 devices: a whole 2x2x4 slice. The times are simulated.
32 devices in a mesh: ctx: 16 (over z, x, core), head: 2 (over y).
Axes of the slice: x: 2, y: 2, z: 4, core: 2. Of those that a mesh axis runs over, the one named last changes fastest.
Arguments:
- queries: bfloat16 [4096, 32, 128], P('ctx', 'head'), may hold values from -300 to 300
- key_rows: bfloat16 [4096, 4, 128], P('ctx', 'head'), may hold values from -6 to 6
- value_vectors: bfloat16 [4096, 4, 128], P('ctx', 'head'), may hold values from -6 to 6
- doc_ids: int32 [4096], replicated, may hold values from 0 to 2, never falling along the last dimension, each value on 1 to 1792 neighbouring positions
Outputs:
- attended: bfloat16 [4096, 32, 128], P(('ctx', 'head'))
Inputs may be any that keep to these rules, and one draw needn't show every extreme that they name: `doc_ids`: ids never fall along the pack and each prompt holds at most 1792 tokens.
All inputs are finite; a program needn't handle non-finite values.
Results may differ from a plain program's by a relative error of at most 0.008.
Values may be sent and summed in bfloat16 or wider, within the bound.
A program may use at most 64 MiB of HBM per device.

v0:
```python
import jax
import jax.numpy as jnp
from jax import lax
from jax.sharding import PartitionSpec as P


def passed_along(block, axis, distance):
    devices = range(lax.axis_size(axis))
    route = [(i - distance, i) for i in devices if i - distance in devices]
    return lax.ppermute(block, axis, route)


def body(queries, key_rows, value_vectors, doc_ids):
    tok_len, heads_here, head_dim = queries.shape
    kv_heads = key_rows.shape[1]
    head_group = heads_here // kv_heads
    inv_root = head_dim ** (-0.5)
    cycle_size = lax.axis_size("ctx")
    reach_blocks = cycle_size // 2 - 1
    ctx_index = lax.axis_index("ctx")
    query_offset = ctx_index * tok_len
    own_doc = lax.dynamic_slice_in_dim(doc_ids, query_offset, tok_len, 0)
    own_pos = query_offset + jnp.arange(tok_len, dtype=jnp.int32)
    q_grouped = queries.reshape(tok_len, kv_heads, head_group, head_dim).transpose(1, 2, 0, 3)

    def attend(state, q_heads, query_doc, query_pos, key_block, value_block, key_start):
        key_len = key_block.shape[0]
        clamped = jnp.maximum(key_start, 0)
        key_doc = lax.dynamic_slice_in_dim(doc_ids, clamped, key_len, 0)
        key_pos = key_start + jnp.arange(key_len, dtype=jnp.int32)
        visible = (
            (query_doc[:, None] == key_doc[None, :])
            & (key_pos[None, :] <= query_pos[:, None])
            & (key_pos[None, :] >= 0)
        )
        key_major = key_block.transpose(1, 0, 2)
        value_major = value_block.transpose(1, 0, 2)

        def per_group(operand):
            q_group, k_group, v_group, run_max, run_sum, run_out = operand
            scores = (
                jnp.einsum("rtd,ud->rtu", q_group, k_group, preferred_element_type=jnp.float32)
                * inv_root
            )
            masked = jnp.where(visible[None], scores, -1e30)
            new_max = jnp.maximum(run_max, jnp.max(masked, axis=-1))
            weights = jnp.where(visible[None], jnp.exp(scores - new_max[..., None]), 0.0)
            rescale = jnp.exp(run_max - new_max)
            new_sum = run_sum * rescale + jnp.sum(weights, axis=-1)
            product = jnp.einsum(
                "rtu,ud->rtd",
                weights.astype(jnp.bfloat16),
                v_group,
                preferred_element_type=jnp.float32,
            )
            new_out = run_out * rescale[..., None] + product
            return (new_max, new_sum, new_out)

        return lax.map(per_group, (q_heads, key_major, value_major) + tuple(tuple(state)))

    state = attend(
        (
            jnp.full((kv_heads, head_group, tok_len), -1e30, jnp.float32),
            jnp.zeros((kv_heads, head_group, tok_len), jnp.float32),
            jnp.zeros((kv_heads, head_group, tok_len, head_dim), jnp.float32),
        ),
        q_grouped,
        own_doc,
        own_pos,
        key_rows,
        value_vectors,
        query_offset,
    )
    window_keys, window_values = (key_rows, value_vectors)
    covered = 1
    while covered < reach_blocks + 1:
        count = min(covered, reach_blocks + 1 - covered)
        arrived = passed_along((window_keys, window_values), "ctx", covered)
        window_keys = jnp.concatenate([arrived[0], window_keys], axis=0)
        window_values = jnp.concatenate([arrived[1], window_values], axis=0)
        covered = covered + count

    def window_turn(shard_num, carry):
        begin = (shard_num * tok_len).astype(jnp.int32)
        key_piece = lax.dynamic_slice_in_dim(window_keys, begin, tok_len, 0)
        value_piece = lax.dynamic_slice_in_dim(window_values, begin, tok_len, 0)
        return attend(
            carry,
            q_grouped,
            own_doc,
            own_pos,
            key_piece,
            value_piece,
            query_offset - (reach_blocks - shard_num) * tok_len,
        )

    state = lax.fori_loop(0, reach_blocks, window_turn, tuple(state))
    finished = (state[2] / state[1][..., None]).astype(jnp.bfloat16)
    merged = finished.transpose(2, 0, 1, 3).reshape(tok_len, heads_here, head_dim)
    return lax.all_to_all(merged, "head", split_axis=0, concat_axis=1, tiled=True)


def solution(mesh):
    placed = (P("ctx", "head", None), P("ctx", "head", None), P("ctx", "head", None), P())
    return jax.shard_map(
        body, mesh=mesh, in_specs=placed, out_specs=P(("ctx", "head"), None, None), check_vma=False
    )
```

profile of v0, /device:TPU:16, one launch (start us, length us, event | category | flops | bytes accessed | tf_op | source)
XLA Modules:
  0.0 104.9 jit_solution(14884595993120103621)
XLA Ops:
  0.0 1.7 %fusion.53 = (bf16[256,2,128]{2,0,1:T(8,128)(2,1)S(1)}, bf16[2,256,128]{2,1,0:T(8,128)(2,1)}, bf16[2,256,128]{2,1,0:T(8,128)(2,1)}, bf16[256,2,128]{2,0,1:T(8,128)(2,1)S(1)}) fusion(bf16[256,2,128]{2,1,0:T(2,128)(2,1)} %param.12, bf16[256,2,128]{2,1,0:T(2,128)(2,1)} %param.11), kind=kLoop, calls=%fused_computation.84 | loop fusion | bytes 786432 | tf_op args[2]
  1.7 1.9 %collective-permute-start = (bf16[256,2,128]{2,0,1:T(8,128)(2,1)S(1)}, bf16[256,2,128]{2,0,1:T(8,128)(2,1)S(1)}, u32[]{:S(2)}, u32[]{:S(2)}) collective-permute-start(bf16[256,2,128]{2,0,1:T(8,128)(2,1)S(1)} %get-tuple-element.557), channel_id=1, source_target_pairs={{0,2},{2,4},{4,6},{6,8},{8,10},{10,12},{12,14},{14,16},{16,18},{18... | collective-permute-start | bytes 393224 | tf_op jit(solution)/shard_map/ppermute | solution.py:10
  3.7 3.5 %collective-permute-start.3 = (bf16[256,2,128]{2,0,1:T(8,128)(2,1)S(1)}, bf16[256,2,128]{2,0,1:T(8,128)(2,1)S(1)}, u32[]{:S(2)}, u32[]{:S(2)}) collective-permute-start(bf16[256,2,128]{2,0,1:T(8,128)(2,1)S(1)} %get-tuple-element.550), channel_id=1, source_target_pairs={{0,2},{2,4},{4,6},{6,8},{8,10},{10,12},{12,14},{14,16},{16,18},{18... | collective-permute-start | bytes 393224 | tf_op jit(solution)/shard_map/ppermute | solution.py:10
  7.2 1.7 %collective-permute-done = bf16[256,2,128]{2,0,1:T(8,128)(2,1)S(1)} collective-permute-done((bf16[256,2,128]{2,0,1:T(8,128)(2,1)S(1)}, bf16[256,2,128]{2,0,1:T(8,128)(2,1)S(1)}, u32[]{:S(2)}, u32[]{:S(2)}) %collective-permute-start) | collective-permute-done | bytes 131104 | tf_op jit(solution)/shard_map/ppermute | solution.py:10
  9.7 2.5 %collective-permute-start.1 = (bf16[512,2,128]{2,0,1:T(8,128)(2,1)}, bf16[512,2,128]{2,0,1:T(8,128)(2,1)}, u32[]{:S(2)}, u32[]{:S(2)}) collective-permute-start(bf16[512,2,128]{2,0,1:T(8,128)(2,1)} %pad_maximum_fusion.4), channel_id=1, source_target_pairs={{0,4},{2,6},{4,8},{6,10},{8,12},{10,14},{12,16},{14,18},{16,20},{1... | collective-permute-start | bytes 786440 | tf_op jit(solution)/shard_map/ppermute | solution.py:10
  12.9 4.3 %collective-permute-start.4 = (bf16[512,2,128]{2,0,1:T(8,128)(2,1)}, bf16[512,2,128]{2,0,1:T(8,128)(2,1)}, u32[]{:S(2)}, u32[]{:S(2)}) collective-permute-start(bf16[512,2,128]{2,0,1:T(8,128)(2,1)} %pad_maximum_fusion.5), channel_id=1, source_target_pairs={{0,4},{2,6},{4,8},{6,10},{8,12},{10,14},{12,16},{14,18},{16,20},{1... | collective-permute-start | bytes 786440 | tf_op jit(solution)/shard_map/ppermute | solution.py:10
  17.3 1.5 %copy.34 = bf16[256,16,128]{2,0,1:T(8,128)(2,1)S(1)} copy(bf16[256,16,128]{2,1,0:T(8,128)(2,1)} %param.10) | data formatting | bytes 2097152 | tf_op args[0]
  18.8 0.9 fusion.55
  19.7 1.3 %collective-permute-done.1 = bf16[512,2,128]{2,0,1:T(8,128)(2,1)} collective-permute-done((bf16[512,2,128]{2,0,1:T(8,128)(2,1)}, bf16[512,2,128]{2,0,1:T(8,128)(2,1)}, u32[]{:S(2)}, u32[]{:S(2)}) %collective-permute-start.1) | collective-permute-done | bytes 262176 | tf_op jit(solution)/shard_map/ppermute | solution.py:10
  20.9 1.8 %pad_maximum_fusion.2 = bf16[1024,2,128]{2,0,1:T(8,128)(2,1)} fusion(bf16[256,2,128]{2,0,1:T(8,128)(2,1)S(1)} %get-tuple-element.557, bf16[256,2,128]{2,0,1:T(8,128)(2,1)} %copy-done.3, bf16[512,2,128]{2,0,1:T(8,128)(2,1)} %collective-permute-done.1), kind=kLoop, calls=%fused_computation.76 | loop fusion | flops 1572864 | bytes 1048576 | tf_op jit(solution)/shard_map/concatenate | solution.py:79
  22.8 4.5 %collective-permute-start.2 = (bf16[1024,2,128]{2,0,1:T(8,128)(2,1)}, bf16[1024,2,128]{2,0,1:T(8,128)(2,1)}, u32[]{:S(2)}, u32[]{:S(2)}) collective-permute-start(bf16[1024,2,128]{2,0,1:T(8,128)(2,1)} %pad_maximum_fusion.2), channel_id=1, source_target_pairs={{0,8},{2,10},{4,12},{6,14},{8,16},{10,18},{12,20},{14,22},{16,24},... | collective-permute-start | bytes 1572872 | tf_op jit(solution)/shard_map/ppermute | solution.py:10
  27.3 1.9 %pad_maximum_fusion.3 = bf16[1024,2,128]{2,0,1:T(8,128)(2,1)} fusion(bf16[256,2,128]{2,0,1:T(8,128)(2,1)S(1)} %get-tuple-element.550, bf16[256,2,128]{2,0,1:T(8,128)(2,1)} %copy-done.1, bf16[512,2,128]{2,0,1:T(8,128)(2,1)} %collective-permute-done.4), kind=kLoop, calls=%fused_computation.77 | loop fusion | flops 1572864 | bytes 1048576 | tf_op jit(solution)/shard_map/concatenate | solution.py:80
  29.1 2.8 %collective-permute-start.5 = (bf16[1024,2,128]{2,0,1:T(8,128)(2,1)}, bf16[1024,2,128]{2,0,1:T(8,128)(2,1)}, u32[]{:S(2)}, u32[]{:S(2)}) collective-permute-start(bf16[1024,2,128]{2,0,1:T(8,128)(2,1)} %pad_maximum_fusion.3), channel_id=1, source_target_pairs={{0,8},{2,10},{4,12},{6,14},{8,16},{10,18},{12,20},{14,22},{16,24},... | collective-permute-start | bytes 1572872 | tf_op jit(solution)/shard_map/ppermute | solution.py:10
  32.0 5.7 %while.66 = (s32[]{:T(128)}, f32[2,8,256]{2,1,0:T(8,128)S(1)}, f32[2,8,256]{2,1,0:T(8,128)S(1)}, f32[2,8,256,128]{3,2,1,0:T(8,128)S(1)}, bf16[2,8,256,128]{3,2,1...) while((s32[]{:T(128)}, f32[2,8,256]{2,1,0:T(8,128)S(1)}, ...), condition=%wide.region_3.4_spmd.clone, body=%wide.region_0.3_spmd.clone.sunk | while | flops 274737152 | bytes 8885661 | solution.py:59
  32.2 1.3 %select_reduce_fusion.4 = (f32[8,256]{1,0:T(8,128)S(1)}, f32[8,256,256]{1,2,0:T(8,128)S(1)}) fusion(pred[256,256]{0,1:T(8,128)(4,1)S(1)} %and_and_fusion.4, bf16[2,256,128]{2,1,0:T(8,128)(2,1)} %get-tuple-element.890, s32[]{:T(128)S(6)} %copy.77, bf16[2,8,256,128]{3,2,1,0:T(8,128)(2,1)S(1)} %get-tuple-element.889), kind=kOutput, calls=%fused_computation.4.clone.1 | convolution fusion | flops 135788544 | bytes 2761728 | tf_op jit(solution)/shard_map/while/body/eval_jaxpr/rtd,ud->rtu/dot_general | solution.py:42
  35.0 1.3 %select_reduce_fusion.4 = (f32[8,256]{1,0:T(8,128)S(1)}, f32[8,256,256]{1,2,0:T(8,128)S(1)}) fusion(pred[256,256]{0,1:T(8,128)(4,1)S(1)} %and_and_fusion.4, bf16[2,256,128]{2,1,0:T(8,128)(2,1)} %get-tuple-element.890, s32[]{:T(128)S(6)} %copy.77, bf16[2,8,256,128]{3,2,1,0:T(8,128)(2,1)S(1)} %get-tuple-element.889), kind=kOutput, calls=%fused_computation.4.clone.1 | convolution fusion | flops 135788544 | bytes 2761728 | tf_op jit(solution)/shard_map/while/body/eval_jaxpr/rtd,ud->rtu/dot_general | solution.py:42
  37.7 2.1 %collective-permute-done.2 = bf16[1024,2,128]{2,0,1:T(8,128)(2,1)} collective-permute-done((bf16[1024,2,128]{2,0,1:T(8,128)(2,1)}, bf16[1024,2,128]{2,0,1:T(8,128)(2,1)}, u32[]{:S(2)}, u32[]{:S(2)}) %collective-permute-start.2) | collective-permute-done | bytes 524320 | tf_op jit(solution)/shard_map/ppermute | solution.py:10
  39.8 2.3 %pad_maximum_fusion = bf16[2048,2,128]{2,0,1:T(8,128)(2,1)} fusion(bf16[256,2,128]{2,0,1:T(8,128)(2,1)} %copy-done, bf16[256,2,128]{2,0,1:T(8,128)(2,1)} %copy-done.3, bf16[512,2,128]{2,0,1:T(8,128)(2,1)} %collective-permute-done.1, bf16[1024,2,128]{2,0,1:T(8,128)(2,1)} %collective-permute-done.2), kind=kLoop, calls=%fused_computation.72 | loop fusion | flops 4194304 | bytes 2097152 | tf_op jit(solution)/shard_map/concatenate | solution.py:79
  42.1 4.5 %collective-permute-done.5 = bf16[1024,2,128]{2,0,1:T(8,128)(2,1)} collective-permute-done((bf16[1024,2,128]{2,0,1:T(8,128)(2,1)}, bf16[1024,2,128]{2,0,1:T(8,128)(2,1)}, u32[]{:S(2)}, u32[]{:S(2)}) %collective-permute-start.5) | collective-permute-done | bytes 524320 | tf_op jit(solution)/shard_map/ppermute | solution.py:10
  46.5 2.2 %pad_maximum_fusion.1 = bf16[2048,2,128]{2,0,1:T(8,128)(2,1)} fusion(bf16[256,2,128]{2,0,1:T(8,128)(2,1)S(1)} %get-tuple-element.550, bf16[256,2,128]{2,0,1:T(8,128)(2,1)S(1)} %copy-done.2, bf16[512,2,128]{2,0,1:T(8,128)(2,1)} %collective-permute-done.4, bf16[1024,2,128]{2,0,1:T(8,128)(2,1)} %collective-permute-done.5), kind=kLoop, calls=%fused_computation.73 | loop fusion | flops 4194304 | bytes 2097152 | tf_op jit(solution)/shard_map/concatenate | solution.py:80
  48.7 41.5 %while.68 = (s32[]{:T(128)}, f32[2,8,256]{2,1,0:T(8,128)S(1)}, f32[2,8,256]{2,1,0:T(8,128)S(1)}, f32[2,8,256,128]{3,2,1,0:T(8,128)S(1)}, bf16[2048,2,128]{2,0,1:...) while((s32[]{:T(128)}, f32[2,8,256]{2,1,0:T(8,128)S(1)}, ...), condition=%wide.region_9.10_spmd.clone.clone, body=%wide.region_4.9_spmd.clone.clone.sunk | while | flops 274998272 | bytes 12061712 | solution.py:97
  48.7 1.0 dynamic-slice_bitcast_fusion.3
  50.5 4.1 %while.69 = (s32[]{:T(128)}, f32[2,8,256]{2,1,0:T(8,128)S(1)}, f32[2,8,256]{2,1,0:T(8,128)S(1)}, f32[2,8,256,128]{3,2,1,0:T(8,128)S(1)}, bf16[2,8,256,128]{3,2,1...) while((s32[]{:T(128)}, f32[2,8,256]{2,1,0:T(8,128)S(1)}, ...), condition=%wide.region_8.8_spmd.clone.clone, body=%wide.region_5.7_spmd.clone.clone.sunk | while | flops 274997248 | bytes 11532689 | solution.py:59
  51.7 0.8 fusion.77
  53.8 0.8 fusion.77
  54.6 1.0 dynamic-slice_bitcast_fusion.3
  56.4 4.1 %while.69 = (s32[]{:T(128)}, f32[2,8,256]{2,1,0:T(8,128)S(1)}, f32[2,8,256]{2,1,0:T(8,128)S(1)}, f32[2,8,256,128]{3,2,1,0:T(8,128)S(1)}, bf16[2,8,256,128]{3,2,1...) while((s32[]{:T(128)}, f32[2,8,256]{2,1,0:T(8,128)S(1)}, ...), condition=%wide.region_8.8_spmd.clone.clone, body=%wide.region_5.7_spmd.clone.clone.sunk | while | flops 274997248 | bytes 11532689 | solution.py:59
  57.7 0.8 fusion.77
  59.7 0.8 fusion.77
  60.6 1.0 dynamic-slice_bitcast_fusion.3
  62.4 4.1 %while.69 = (s32[]{:T(128)}, f32[2,8,256]{2,1,0:T(8,128)S(1)}, f32[2,8,256]{2,1,0:T(8,128)S(1)}, f32[2,8,256,128]{3,2,1,0:T(8,128)S(1)}, bf16[2,8,256,128]{3,2,1...) while((s32[]{:T(128)}, f32[2,8,256]{2,1,0:T(8,128)S(1)}, ...), condition=%wide.region_8.8_spmd.clone.clone, body=%wide.region_5.7_spmd.clone.clone.sunk | while | flops 274997248 | bytes 11532689 | solution.py:59
  63.6 0.8 fusion.77
  65.7 0.8 fusion.77
  66.5 1.0 dynamic-slice_bitcast_fusion.3
  68.3 4.1 %while.69 = (s32[]{:T(128)}, f32[2,8,256]{2,1,0:T(8,128)S(1)}, f32[2,8,256]{2,1,0:T(8,128)S(1)}, f32[2,8,256,128]{3,2,1,0:T(8,128)S(1)}, bf16[2,8,256,128]{3,2,1...) while((s32[]{:T(128)}, f32[2,8,256]{2,1,0:T(8,128)S(1)}, ...), condition=%wide.region_8.8_spmd.clone.clone, body=%wide.region_5.7_spmd.clone.clone.sunk | while | flops 274997248 | bytes 11532689 | solution.py:59
  69.6 0.8 fusion.77
  71.6 0.8 fusion.77
  72.5 1.0 dynamic-slice_bitcast_fusion.3
  74.3 4.1 %while.69 = (s32[]{:T(128)}, f32[2,8,256]{2,1,0:T(8,128)S(1)}, f32[2,8,256]{2,1,0:T(8,128)S(1)}, f32[2,8,256,128]{3,2,1,0:T(8,128)S(1)}, bf16[2,8,256,128]{3,2,1...) while((s32[]{:T(128)}, f32[2,8,256]{2,1,0:T(8,128)S(1)}, ...), condition=%wide.region_8.8_spmd.clone.clone, body=%wide.region_5.7_spmd.clone.clone.sunk | while | flops 274997248 | bytes 11532689 | solution.py:59
  75.5 0.8 fusion.77
  77.6 0.8 fusion.77
  78.4 1.0 dynamic-slice_bitcast_fusion.3
  80.2 4.1 %while.69 = (s32[]{:T(128)}, f32[2,8,256]{2,1,0:T(8,128)S(1)}, f32[2,8,256]{2,1,0:T(8,128)S(1)}, f32[2,8,256,128]{3,2,1,0:T(8,128)S(1)}, bf16[2,8,256,128]{3,2,1...) while((s32[]{:T(128)}, f32[2,8,256]{2,1,0:T(8,128)S(1)}, ...), condition=%wide.region_8.8_spmd.clone.clone, body=%wide.region_5.7_spmd.clone.clone.sunk | while | flops 274997248 | bytes 11532689 | solution.py:59
  84.3 1.0 dynamic-slice_bitcast_fusion.3
  86.1 4.1 %while.69 = (s32[]{:T(128)}, f32[2,8,256]{2,1,0:T(8,128)S(1)}, f32[2,8,256]{2,1,0:T(8,128)S(1)}, f32[2,8,256,128]{3,2,1,0:T(8,128)S(1)}, bf16[2,8,256,128]{3,2,1...) while((s32[]{:T(128)}, f32[2,8,256]{2,1,0:T(8,128)S(1)}, ...), condition=%wide.region_8.8_spmd.clone.clone, body=%wide.region_5.7_spmd.clone.clone.sunk | while | flops 274997248 | bytes 11532689 | solution.py:59
  87.4 0.8 fusion.77
  91.7 12.1 %all_to_all.18 = bf16[256,16,128]{2,1,0:T(8,128)(2,1)S(1)} all-to-all(bf16[256,16,128]{2,1,0:T(8,128)(2,1)S(1)} %bitcast.122), channel_id=1, replica_groups=mesh['ctx'=16,'head'=2] {'head'}, dimensions={0} | all-to-all | bytes 2097152 | tf_op jit(solution)/shard_map/all_to_all | solution.py:100
  103.8 1.1 %copy.46 = bf16[128,2,16,128]{3,2,1,0:T(8,128)(2,1)} copy(bf16[128,2,16,128]{3,2,0,1:T(8,128)(2,1)S(1)} %bitcast.123) | data formatting | bytes 2097152 | tf_op jit(solution)/shard_map/all_to_all | solution.py:100
  (141 shorter events, 30.3 us)
Async XLA Ops:
  1.7 21.1 %copy-start = (bf16[256,2,128]{2,0,1:T(8,128)(2,1)}, bf16[256,2,128]{2,0,1:T(8,128)(2,1)S(1)}, u32[]{:S(2)}) copy-start(bf16[256,2,128]{2,0,1:T(8,128)(2,1)S(1)} %get-tuple-element.557) | copy-start | bytes 393220
  1.7 7.2 %collective-permute-start = (bf16[256,2,128]{2,0,1:T(8,128)(2,1)S(1)}, bf16[256,2,128]{2,0,1:T(8,128)(2,1)S(1)}, u32[]{:S(2)}, u32[]{:S(2)}) collective-permute-start(bf16[256,2,128]{2,0,1:T(8,128)(2,1)S(1)} %get-tuple-element.557), channel_id=1, source_target_pairs={{0,2},{2,4},{4,6},{6,8},{8,10},{10,12},{12,14},{14,16},{16,18},{18... | collective-permute-start | bytes 393224 | tf_op jit(solution)/shard_map/ppermute | solution.py:10
  3.7 8.5 %collective-permute-start.3 = (bf16[256,2,128]{2,0,1:T(8,128)(2,1)S(1)}, bf16[256,2,128]{2,0,1:T(8,128)(2,1)S(1)}, u32[]{:S(2)}, u32[]{:S(2)}) collective-permute-start(bf16[256,2,128]{2,0,1:T(8,128)(2,1)S(1)} %get-tuple-element.550), channel_id=1, source_target_pairs={{0,2},{2,4},{4,6},{6,8},{8,10},{10,12},{12,14},{14,16},{16,18},{18... | collective-permute-start | bytes 393224 | tf_op jit(solution)/shard_map/ppermute | solution.py:10
  8.9 8.4 %copy-start.3 = (bf16[256,2,128]{2,0,1:T(8,128)(2,1)}, bf16[256,2,128]{2,0,1:T(8,128)(2,1)S(1)}, u32[]{:S(2)}) copy-start(bf16[256,2,128]{2,0,1:T(8,128)(2,1)S(1)} %collective-permute-done) | copy-start | bytes 393220
  9.7 11.3 %collective-permute-start.1 = (bf16[512,2,128]{2,0,1:T(8,128)(2,1)}, bf16[512,2,128]{2,0,1:T(8,128)(2,1)}, u32[]{:S(2)}, u32[]{:S(2)}) collective-permute-start(bf16[512,2,128]{2,0,1:T(8,128)(2,1)} %pad_maximum_fusion.4), channel_id=1, source_target_pairs={{0,4},{2,6},{4,8},{6,10},{8,12},{10,14},{12,16},{14,18},{16,20},{1... | collective-permute-start | bytes 786440 | tf_op jit(solution)/shard_map/ppermute | solution.py:10
  12.2 5.1 %copy-start.1 = (bf16[256,2,128]{2,0,1:T(8,128)(2,1)}, bf16[256,2,128]{2,0,1:T(8,128)(2,1)S(1)}, u32[]{:S(2)}) copy-start(bf16[256,2,128]{2,0,1:T(8,128)(2,1)S(1)} %collective-permute-done.3) | copy-start | bytes 393220
  12.9 14.4 %collective-permute-start.4 = (bf16[512,2,128]{2,0,1:T(8,128)(2,1)}, bf16[512,2,128]{2,0,1:T(8,128)(2,1)}, u32[]{:S(2)}, u32[]{:S(2)}) collective-permute-start(bf16[512,2,128]{2,0,1:T(8,128)(2,1)} %pad_maximum_fusion.5), channel_id=1, source_target_pairs={{0,4},{2,6},{4,8},{6,10},{8,12},{10,14},{12,16},{14,18},{16,20},{1... | collective-permute-start | bytes 786440 | tf_op jit(solution)/shard_map/ppermute | solution.py:10
  22.8 17.0 %collective-permute-start.2 = (bf16[1024,2,128]{2,0,1:T(8,128)(2,1)}, bf16[1024,2,128]{2,0,1:T(8,128)(2,1)}, u32[]{:S(2)}, u32[]{:S(2)}) collective-permute-start(bf16[1024,2,128]{2,0,1:T(8,128)(2,1)} %pad_maximum_fusion.2), channel_id=1, source_target_pairs={{0,8},{2,10},{4,12},{6,14},{8,16},{10,18},{12,20},{14,22},{16,24},... | collective-permute-start | bytes 1572872 | tf_op jit(solution)/shard_map/ppermute | solution.py:10
  29.1 17.4 %collective-permute-start.5 = (bf16[1024,2,128]{2,0,1:T(8,128)(2,1)}, bf16[1024,2,128]{2,0,1:T(8,128)(2,1)}, u32[]{:S(2)}, u32[]{:S(2)}) collective-permute-start(bf16[1024,2,128]{2,0,1:T(8,128)(2,1)} %pad_maximum_fusion.3), channel_id=1, source_target_pairs={{0,8},{2,10},{4,12},{6,14},{8,16},{10,18},{12,20},{14,22},{16,24},... | collective-permute-start | bytes 1572872 | tf_op jit(solution)/shard_map/ppermute | solution.py:10
  32.2 1.9 %copy-start.4 = (bf16[2,256,128]{2,1,0:T(8,128)(2,1)S(1)}, bf16[2,256,128]{2,1,0:T(8,128)(2,1)}, u32[]{:S(2)}) copy-start(bf16[2,256,128]{2,1,0:T(8,128)(2,1)} %get-tuple-element.891) | copy-start | bytes 393220 | tf_op jit(solution)/shard_map/while
  35.0 1.8 %copy-start.4 = (bf16[2,256,128]{2,1,0:T(8,128)(2,1)S(1)}, bf16[2,256,128]{2,1,0:T(8,128)(2,1)}, u32[]{:S(2)}) copy-start(bf16[2,256,128]{2,1,0:T(8,128)(2,1)} %get-tuple-element.891) | copy-start | bytes 393220 | tf_op jit(solution)/shard_map/while
  37.7 8.9 %copy-start.2 = (bf16[256,2,128]{2,0,1:T(8,128)(2,1)S(1)}, bf16[256,2,128]{2,0,1:T(8,128)(2,1)}, u32[]{:S(2)}) copy-start(bf16[256,2,128]{2,0,1:T(8,128)(2,1)} %copy-done.1) | copy-start | bytes 393220
where the time goes:
time: 107 us; the launch traced here: 105 us
  matrix products  22 us (21%)
  other arithmetic  20.8 us (19%)
  starting transfers between devices  19.6 us (18%)
  local copies, waits for them, and re-layouts  19.4 us (18%)
  blocking collectives  12.1 us (11%)
  waiting for transfers between devices  9.53 us (9%)
  loops' own time  1.35 us (1%)
    ppermute x6, starting transfers between devices, passed_along(): return lax.ppermute(block, axis, route)  19.6 us
    dot_general x16, matrix products, per_group(): jnp.einsum('rtu,ud->rtd', weights.astype(jnp.bfloat16), v_group, preferre...  12.8 us
    all_to_all x1, blocking collectives, body(): lax.all_to_all(merged, 'head', split_axis=0, concat_axis=1, tiled=True)  12.1 us
    ppermute x6, waiting for transfers between devices, passed_along(): return lax.ppermute(block, axis, route)  9.53 us
    dot_general x16, matrix products, per_group(): jnp.einsum('rtd,ud->rtu', q_group, k_group, preferred_element_type=jnp.fl...  9.2 us
    reduce_sum x16, other arithmetic, per_group(): new_sum = run_sum * rescale + jnp.sum(weights, axis=-1)  7.09 us
    transpose x7, local copies, waits for them, and re-layouts, attend(): value_major = value_block.transpose(1, 0, 2)  6.97 us
    dynamic_slice x7, local copies, waits for them, and re-layouts, attend(): key_doc = lax.dynamic_slice_in_dim(doc_ids, clamped, key_len, 0)  5.45 us
  transfers between devices with their start and end apart: 6, of which 4 were waited for; matrix products, arithmetic and copies ran while one was open for 15% of the time, Pallas kernels for 0%

commit v1 on v0

v1 whole, which is shorter than its diff:
```python
import functools
import math

import jax
import jax.numpy as jnp
from jax import lax
from jax.experimental import pallas as pl
from jax.experimental.pallas import tpu as pltpu
from jax.sharding import PartitionSpec as P

MESH = pl.DeviceIdType.MESH
MEMBERS = 4
CHUNK_BLOCKS = 4
ROWS = 256
HIDDEN = -1e30


def kernel(n, q_ref, kv_ref, start_ref, out_ref, win, q_scr, start_scr, done,
           ring_send, pair_send, core_send, recv, local_sem, out_send, out_recv):
    reach = n // 2 - 1
    groups = n // MEMBERS
    depth = -(-reach // MEMBERS)
    kv_heads = kv_ref.shape[0]
    tok_len = q_ref.shape[0]
    head_dim = q_ref.shape[2]
    group_heads = q_ref.shape[1] // kv_heads
    half = tok_len // 2
    scale = head_dim ** (-0.5) * math.log2(math.e)

    i = lax.axis_index("ctx")
    y = lax.axis_index("head")
    g = i // MEMBERS
    j = i % MEMBERS
    x = j // 2
    k = j % 2
    own = MEMBERS * depth + j
    first = own - reach
    after = lax.rem(i + MEMBERS, n)
    before = lax.rem(i + n - MEMBERS, n)
    pair = i + 2 - 4 * x
    sibling = i + 1 - 2 * k

    barrier = pltpu.get_barrier_semaphore()
    for target in (after, before, pair, sibling):
        pl.semaphore_signal(barrier, inc=1, device_id={"ctx": target}, device_id_type=MESH)
    pl.semaphore_signal(barrier, inc=1, device_id={"head": 1 - y}, device_id_type=MESH)
    pl.semaphore_wait(barrier, 5)

    def slot(s, m):
        return MEMBERS * (depth - s) + m

    def copy(src, lin, h, sem, target):
        return pltpu.make_async_remote_copy(
            src_ref=src, dst_ref=win.at[lin, h], send_sem=sem, recv_sem=recv.at[lin, h],
            device_id={"ctx": target}, device_id_type=MESH)

    def source(s, m, h):
        return kv_ref.at[h] if s is None else win.at[slot(s, m), h]

    base = MEMBERS * depth

    def ring_wanted(s):
        return slot(s, j) >= base - reach

    def pair_wanted(s, m, chip):
        lin = slot(s, m)
        return (lin >= base + 2 * chip - reach) & (lin < base + 2 * chip) & (g >= s)

    def core_wanted(s, m, core):
        lin = slot(s, m)
        mine = base + 2 * x + core
        return (lin >= mine - reach) & (lin < mine) & (g >= s)

    def send_ring(s, h, src, act):
        @pl.when((g + 1 < groups) & (g >= s) & ring_wanted(s + 1))
        def _():
            c = copy(src, slot(s + 1, j), h, ring_send.at[s, h], after)
            act(c)

    def send_pair(s, h, src, act):
        @pl.when(pair_wanted(s, j, 1 - x))
        def _():
            act(copy(src, slot(s, j), h, pair_send.at[s, h], pair))

    def send_core(s, m, way, h, src, act):
        @pl.when(core_wanted(s, m, 1 - k))
        def _():
            act(copy(src, slot(s, m), h, core_send.at[way, s, h], sibling))

    def start(c):
        c.start()

    def wait_sent(c):
        c.wait_send()

    def wait_slot(lin, h):
        copy(win.at[lin, h], lin, h, ring_send.at[0, h], sibling).wait_recv()

    def pump_own(h):
        send_ring(0, h, kv_ref.at[h], start)
        send_pair(0, h, kv_ref.at[h], start)
        send_core(0, j, 0, h, kv_ref.at[h], start)

    def pump_ring(s, h):
        @pl.when((g >= s) & ring_wanted(s))
        def _():
            wait_slot(slot(s, j), h)
        src = win.at[slot(s, j), h]
        if s < depth:
            send_ring(s, h, src, start)
        send_pair(s, h, src, start)
        send_core(s, j, 0, h, src, start)

    def pump_pair(s, h):
        m = j + 2 - 4 * x

        @pl.when(pair_wanted(s, m, x))
        def _():
            wait_slot(slot(s, m), h)
        send_core(s, m, 1, h, win.at[slot(s, m), h], start)

    def pump_core(h):
        for s in range(depth + 1):
            for m in (j + 1 - 2 * k, 3 - j):
                @pl.when(core_wanted(s, m, k))
                def _():
                    wait_slot(slot(s, m), h)

    def stages(h):
        result = []
        for s in range(1, depth + 1):
            result.append(functools.partial(pump_ring, s, h))
            result.append(functools.partial(pump_pair, s - 1, h))
        result.append(functools.partial(pump_pair, depth, h))
        result.append(functools.partial(pump_core, h))
        return result

    for h in range(kv_heads):
        pump_own(h)
        pltpu.make_async_copy(kv_ref.at[h], win.at[own, h], local_sem.at[h]).start()

    def clear(d, _):
        @pl.when(i < d)
        def _():
            win[own - d] = jnp.zeros(win.shape[1:], win.dtype)
        return 0
    lax.fori_loop(1, reach + 1, clear, 0)

    rows_total = tok_len * group_heads
    toks = ROWS // group_heads

    def prepare(b, _):
        t = pl.multiple_of(b * toks, toks)
        r = pl.multiple_of(b * ROWS, ROWS)
        q = q_ref[pl.ds(t, toks)].astype(jnp.float32)
        for h in range(kv_heads):
            part = q[:, h * group_heads:(h + 1) * group_heads].reshape(ROWS, head_dim)
            q_scr[h, pl.ds(r, ROWS), :] = part.astype(q_scr.dtype)
        st = start_ref[pl.ds(t, toks), :]
        start_scr[pl.ds(r, ROWS), :] = jnp.broadcast_to(
            st[:, None, :], (toks, group_heads, 128)).reshape(ROWS, 128)
        return 0
    lax.fori_loop(0, rows_total // ROWS, prepare, 0)

    chunks = (reach + 1) // CHUNK_BLOCKS
    width = CHUNK_BLOCKS * tok_len
    lane = lax.broadcasted_iota(jnp.int32, (ROWS, 128), 1)
    row_tok = lax.broadcasted_iota(jnp.int32, (ROWS, 128), 0) // group_heads

    def attend(h, r, chunk, newest, state):
        q = q_scr[h, pl.ds(r, ROWS), :]
        begin = first + chunk * CHUNK_BLOCKS
        key_base = (i - reach + chunk * CHUNK_BLOCKS) * tok_len
        st = start_scr[pl.ds(r, ROWS), :] - key_base - lane
        tiles = []
        for b in range(CHUNK_BLOCKS):
            keys = win[begin + b, h, 0]
            s = lax.dot_general(q, keys, (((1,), (1,)), ((), ())),
                                preferred_element_type=jnp.float32)
            for c in range(tok_len // 128):
                off = b * tok_len + c * 128
                tile = s[:, c * 128:(c + 1) * 128]
                seen = st <= off
                if newest and b == CHUNK_BLOCKS - 1:
                    seen = seen & (lane + c * 128 <= row_tok + r // group_heads)
                tiles.append(jnp.where(seen, tile, HIDDEN))
        top = functools.reduce(jnp.maximum, tiles)
        top = jnp.max(top, axis=1, keepdims=True)
        if state is not None:
            top = jnp.maximum(top, state[0])
        weights = [jnp.exp2((t - top) * scale) for t in tiles]
        total = functools.reduce(jnp.add, weights)
        values = win[pl.ds(begin, CHUNK_BLOCKS), h, 1].reshape(width, head_dim)
        packed = jnp.concatenate([w.astype(jnp.bfloat16) for w in weights], axis=1)
        product = jnp.dot(packed, values, preferred_element_type=jnp.float32)
        if state is None:
            return top, total, product
        rescale = jnp.exp2((state[0] - top) * scale)
        return top, state[1] * rescale + total, state[2] * rescale + product

    def block(h, r):
        state = attend(h, r, chunks - 1, True, None)
        if chunks == 2:
            state = attend(h, r, 0, False, state)
        else:
            state = lax.fori_loop(
                1, chunks, lambda c, st: attend(h, r, chunks - 1 - c, False, st), state)
        total = jnp.sum(state[1], axis=1, keepdims=True)
        return (state[2] / total).reshape(toks, group_heads, head_dim).astype(jnp.bfloat16)

    blocks_half = half // toks

    def rows_of(h, token0, dst, b):
        t = pl.multiple_of(token0 + b * toks, toks)
        r = pl.multiple_of(t * group_heads, ROWS)
        dst(pl.multiple_of(b * toks, toks), block(h, r))

    def store_sent(h, t, value):
        done[h, pl.ds(t, toks)] = value

    def store_own(h, t, value):
        out_ref[y, h, pl.ds(t, toks)] = value

    def out_copy(h):
        return pltpu.make_async_remote_copy(
            src_ref=done.at[h], dst_ref=out_ref.at[y, h], send_sem=out_send.at[h],
            recv_sem=out_recv.at[h], device_id={"head": 1 - y}, device_id_type=MESH)

    for h in range(kv_heads):
        pltpu.make_async_copy(kv_ref.at[h], win.at[own, h], local_sem.at[h]).wait()
    for stage in stages(0):
        stage()
    for h in range(kv_heads):
        pending = stages(h + 1) if h + 1 < kv_heads else []
        per = -(-len(pending) // (2 * blocks_half))
        for part, (token0, store) in enumerate(
                (((1 - y) * half, store_sent), (y * half, store_own))):
            if pending:
                for b in range(blocks_half):
                    rows_of(h, token0, functools.partial(store, h), b)
                    for stage in pending[:per]:
                        stage()
                    pending = pending[per:]
            else:
                def step(b, _):
                    rows_of(h, token0, functools.partial(store, h), b)
                    return 0
                lax.fori_loop(0, blocks_half, step, 0)
            if part == 0:
                out_copy(h).start()
        for stage in pending:
            stage()

    for h in range(kv_heads):
        send_ring(0, h, kv_ref.at[h], wait_sent)
        for s in range(depth + 1):
            src = win.at[slot(s, j), h]
            if 0 < s < depth:
                send_ring(s, h, src, wait_sent)
            send_pair(s, h, src, wait_sent)
            send_core(s, j, 0, h, src, wait_sent)
            m = j + 2 - 4 * x
            send_core(s, m, 1, h, win.at[slot(s, m), h], wait_sent)
        out_copy(h).wait()


def body(n, queries, key_rows, value_vectors, doc_ids):
    tok_len, heads_here, head_dim = queries.shape
    kv_heads = key_rows.shape[1]
    group_heads = heads_here // kv_heads
    reach = n // 2 - 1
    depth = -(-reach // MEMBERS)
    slots = MEMBERS * (depth + 1)
    kv = jnp.stack([key_rows, value_vectors]).transpose(2, 0, 1, 3)
    i = lax.axis_index("ctx")
    own_doc = lax.dynamic_slice_in_dim(doc_ids, i * tok_len, tok_len, 0)
    begins = jnp.sum((doc_ids[None, :] < own_doc[:, None]).astype(jnp.int32), axis=1)
    begins = jnp.broadcast_to(begins[:, None], (tok_len, 128))
    half = tok_len // 2
    dma = pltpu.SemaphoreType.DMA
    out = pl.pallas_call(
        functools.partial(kernel, n),
        out_shape=jax.ShapeDtypeStruct(
            (2, kv_heads, half, group_heads, head_dim), jnp.bfloat16),
        in_specs=[pl.BlockSpec(memory_space=pltpu.VMEM)] * 3,
        out_specs=pl.BlockSpec(memory_space=pltpu.VMEM),
        scratch_shapes=[
            pltpu.VMEM((slots, kv_heads, 2, tok_len, head_dim), jnp.bfloat16),
            pltpu.VMEM((kv_heads, tok_len * group_heads, head_dim), jnp.bfloat16),
            pltpu.VMEM((tok_len * group_heads, 128), jnp.int32),
            pltpu.VMEM((kv_heads, half, group_heads, head_dim), jnp.bfloat16),
            dma((depth, kv_heads)),
            dma((depth + 1, kv_heads)),
            dma((2, depth + 1, kv_heads)),
            dma((slots, kv_heads)),
            dma((kv_heads,)),
            dma((kv_heads,)),
            dma((kv_heads,)),
        ],
        compiler_params=pltpu.CompilerParams(collective_id=0, has_side_effects=True),
    )(queries, kv, begins)
    return out.transpose(2, 0, 1, 3, 4).reshape(half, 2 * heads_here, head_dim)


def solution(mesh):
    placed = (P("ctx", "head", None), P("ctx", "head", None), P("ctx", "head", None), P())
    return jax.shard_map(
        functools.partial(body, mesh.shape["ctx"]), mesh=mesh, in_specs=placed,
        out_specs=P(("ctx", "head"), None, None), check_vma=False,
    )
```

time: 107 us -> 50 us (0.47); the launches traced: 105 us -> 49.4 us
  Pallas kernels: 0 us -> 42.5 us
  matrix products: 22 us -> 0 us
  starting transfers between devices: 19.6 us -> 0 us
  other arithmetic: 20.8 us -> 2 us
  local copies, waits for them, and re-layouts: 19.4 us -> 4.89 us
  blocking collectives: 12.1 us -> 0 us
  waiting for transfers between devices: 9.53 us -> 0 us
  loops' own time: 1.35 us -> 0 us
    pallas_call x0 -> x1, Pallas kernels: none -> 42.5 us  [body(): pl.pallas_call(functools.partial(kernel, n), out_shape=jax.ShapeDtypeStru...]
    dot_general x32 -> x0, matrix products: 22 us -> none  [the longest x16 12.8 us: per_group(): jnp.einsum('rtu,ud->rtd', weights.astype(jnp.bfloat16), v_group, preferre...]
    ppermute x6 -> x0, starting transfers between devices: 19.6 us -> none  [passed_along(): return lax.ppermute(block, axis, route)]
    all_to_all x1 -> x0, blocking collectives: 12.1 us -> none  [body(): lax.all_to_all(merged, 'head', split_axis=0, concat_axis=1, tiled=True)]
    concatenate x6 -> x0, other arithmetic: 9.65 us -> none  [the longest x3 4.89 us: body(): window_keys = jnp.concatenate([arrived[0], window_keys], axis=0)]
    ppermute x6 -> x0, waiting for transfers between devices: 9.53 us -> none  [passed_along(): return lax.ppermute(block, axis, route)]
    dynamic_slice x22 -> x1, local copies, waits for them, and re-layouts: 7.37 us -> 0.76 us  [body(): own_doc = lax.dynamic_slice_in_dim(doc_ids, i * tok_len, tok_len, 0)]
    reduce_sum x16 -> x1, other arithmetic: 7.09 us -> 1.28 us  [body(): jnp.sum((doc_ids[None, :] < own_doc[:, None]).astype(jnp.int32), axis=1)]
  transfers between devices with their start and end apart: 6 -> 0, of which waited for: 4 -> 0; matrix products, arithmetic and copies ran while one was open for 15% -> 0% of each run, Pallas kernels for 0% -> 0%
where the time goes in v1:
time: 50 us; the launch traced here: 49.4 us
  Pallas kernels  42.5 us (85%)
  local copies, waits for them, and re-layouts  4.89 us (10%)
  other arithmetic  2 us (4%)
    pallas_call x1, Pallas kernels, body(): pl.pallas_call(functools.partial(kernel, n), out_shape=jax.ShapeDtypeStru...  42.5 us
    transpose x1, local copies, waits for them, and re-layouts, body(): return out.transpose(2, 0, 1, 3, 4).reshape(half, 2 * heads_here, head_dim)  2.37 us
    reduce_sum x1, other arithmetic, body(): jnp.sum((doc_ids[None, :] < own_doc[:, None]).astype(jnp.int32), axis=1)  1.28 us
    another operation x1, local copies, waits for them, and re-layouts, body(): kv = jnp.stack([key_rows, value_vectors]).transpose(2, 0, 1, 3)  1 us

profile of v1, /device:TPU:16, one launch (start us, length us, event | category | flops | bytes accessed | tf_op | source)
XLA Modules:
  0.0 49.4 jit_solution(2920088066990692729)
XLA Ops:
  0.0 0.8 %dynamic_slice.3 = s32[256]{0:T(256)S(1)} dynamic-slice(s32[4096]{0:T(1024)} %param.7, s32[]{:T(128)S(6)} %select_n.3), dynamic_slice_sizes={256} | dynamic-slice | bytes 2052 | tf_op jit(solution)/shard_map/dynamic_slice | solution.py:276
  0.8 1.3 %convert_reduce_fusion = s32[256]{0:T(256)S(1)} fusion(s32[4096]{0:T(1024)} %param.7, s32[256]{0:T(256)S(1)} %dynamic_slice.3), kind=kLoop, calls=%fused_computation | loop fusion | flops 3145472 | bytes 18432 | tf_op jit(solution)/shard_map/reduce_sum | solution.py:277
  2.0 0.8 %broadcast_in_dim.2.start_ref = s32[256,128]{1,0:T(8,128)} broadcast(s32[256]{0:T(256)S(1)} %convert_reduce_fusion), dimensions={0} | broadcast | bytes 132096 | tf_op jit(solution)/shard_map/broadcast_in_dim | solution.py:278
  2.8 1.0 %copy_bitcast_fusion = (bf16[1,256,2,128]{3,1,0,2:T(8,128)(2,1)S(1)}, bf16[1,256,2,128]{3,1,0,2:T(8,128)(2,1)S(1)}) fusion(bf16[256,2,128]{2,1,0:T(2,128)(2,1)} %param.6, bf16[256,2,128]{2,1,0:T(2,128)(2,1)} %param.5), kind=kLoop, calls=%fused_computation.2 | loop fusion | bytes 524288 | tf_op jit(solution)/shard_map/stack | solution.py:274
  3.8 0.7 %maximum_bitcast_fusion.kv_ref = bf16[2,2,256,128]{3,2,1,0:T(8,128)(2,1)} fusion(bf16[1,256,2,128]{3,1,0,2:T(8,128)(2,1)S(1)} %get-tuple-element.5, bf16[1,256,2,128]{3,1,0,2:T(8,128)(2,1)S(1)} %get-tuple-element.6), kind=kLoop, calls=%fused_computation.1 | loop fusion | flops 131072 | bytes 524288 | tf_op jit(solution)/shard_map/transpose | solution.py:274
  4.5 42.5 %shard_map.46 = bf16[2,2,128,8,128]{4,3,2,1,0:T(8,128)(2,1)} custom-call(bf16[256,16,128]{2,1,0:T(8,128)(2,1)} %q_ref.1, bf16[2,2,256,128]{3,2,1,0:T(8,128)(2,1)} %maximum_bitcast_fusion.kv_ref, s32[256,128]{1,0:T(8,128)} %broadcast_in_dim.2.start_ref), custom_call_target="tpu_custom_call" | custom-call | tf_op jit(solution)/shard_map/pallas_call | solution.py:281
  47.0 2.4 %copy.12 = bf16[128,2,2,8,128]{4,3,2,1,0:T(8,128)(2,1)} copy(bf16[128,2,2,8,128]{4,3,0,2,1:T(8,128)(2,1)} %bitcast.8) | data formatting | bytes 2097152 | tf_op jit(solution)/shard_map/transpose | solution.py:302

commit v2 on v1

--- a/solution.py
+++ b/solution.py
@@ -11,16 +11,17 @@
 MESH = pl.DeviceIdType.MESH
 MEMBERS = 4
 CHUNK_BLOCKS = 4
-ROWS = 256
+ROWS = 512
 HIDDEN = -1e30
 
 
-def kernel(n, q_ref, kv_ref, start_ref, out_ref, win, q_scr, start_scr, done,
+def kernel(n, q_ref, kv_ref, docs_ref, out_ref, win, q_scr, start_tok, start_scr, done, top_scr, total_scr, sum_scr,
            ring_send, pair_send, core_send, recv, local_sem, out_send, out_recv):
     reach = n // 2 - 1
     groups = n // MEMBERS
     depth = -(-reach // MEMBERS)
-    kv_heads = kv_ref.shape[0]
+    pieces = kv_ref.shape[0]
+    kv_heads = pieces // 2
     tok_len = q_ref.shape[0]
     head_dim = q_ref.shape[2]
     group_heads = q_ref.shape[1] // kv_heads
@@ -119,25 +120,28 @@
             wait_slot(slot(s, m), h)
         send_core(s, m, 1, h, win.at[slot(s, m), h], start)
 
-    def pump_core(h):
-        for s in range(depth + 1):
-            for m in (j + 1 - 2 * k, 3 - j):
-                @pl.when(core_wanted(s, m, k))
-                def _():
-                    wait_slot(slot(s, m), h)
+    def pump_core(s, h):
+        for m in (j + 1 - 2 * k, 3 - j):
+            @pl.when(core_wanted(s, m, k))
+            def _():
+                wait_slot(slot(s, m), h)
+
+    def both(act, s, h):
+        return [functools.partial(act, s, 2 * h), functools.partial(act, s, 2 * h + 1)]
 
     def stages(h):
-        result = []
-        for s in range(1, depth + 1):
-            result.append(functools.partial(pump_ring, s, h))
-            result.append(functools.partial(pump_pair, s - 1, h))
-        result.append(functools.partial(pump_pair, depth, h))
-        result.append(functools.partial(pump_core, h))
-        return result
-
-    for h in range(kv_heads):
-        pump_own(h)
-        pltpu.make_async_copy(kv_ref.at[h], win.at[own, h], local_sem.at[h]).start()
+        early = (both(pump_ring, 1, h) + both(pump_pair, 0, h) + both(pump_pair, 1, h)
+                 + both(pump_core, 0, h) + both(pump_core, 1, h))
+        late = []
+        for s in range(2, depth + 1):
+            late += [both(pump_ring, s, h), both(pump_pair, s, h)]
+        late += [sum([both(pump_core, s, h) for s in range(2, depth + 1)], [])]
+        return early, late
+
+    for p in range(pieces):
+        pltpu.make_async_copy(kv_ref.at[p], win.at[own, p], local_sem.at[p]).start()
+    for p in range(2):
+        pump_own(p)
 
     def clear(d, _):
         @pl.when(i < d)
@@ -148,6 +152,18 @@
 
     rows_total = tok_len * group_heads
     toks = ROWS // group_heads
+
+    for c in range(tok_len // 128):
+        ids = docs_ref[pl.ds(i * (tok_len // 128) + c, 1), :].astype(jnp.float32)
+        mine = jnp.broadcast_to(ids, (128, 128)).T
+
+        def count(r, smaller):
+            other = docs_ref[pl.ds(r, 1), :].astype(jnp.float32)
+            return smaller + jnp.where(other < mine, 1.0, 0.0)
+        smaller = lax.fori_loop(
+            0, docs_ref.shape[0], count, jnp.zeros((128, 128), jnp.float32), unroll=4)
+        begin_at = jnp.sum(smaller, axis=1, keepdims=True).astype(jnp.int32)
+        start_tok[pl.ds(c * 128, 128), :] = jnp.broadcast_to(begin_at, (128, 128))
 
     def prepare(b, _):
         t = pl.multiple_of(b * toks, toks)
@@ -156,7 +172,7 @@
         for h in range(kv_heads):
             part = q[:, h * group_heads:(h + 1) * group_heads].reshape(ROWS, head_dim)
             q_scr[h, pl.ds(r, ROWS), :] = part.astype(q_scr.dtype)
-        st = start_ref[pl.ds(t, toks), :]
+        st = start_tok[pl.ds(t, toks), :]
         start_scr[pl.ds(r, ROWS), :] = jnp.broadcast_to(
             st[:, None, :], (toks, group_heads, 128)).reshape(ROWS, 128)
         return 0
@@ -174,7 +190,7 @@
         st = start_scr[pl.ds(r, ROWS), :] - key_base - lane
         tiles = []
         for b in range(CHUNK_BLOCKS):
-            keys = win[begin + b, h, 0]
+            keys = win[begin + b, 2 * h]
             s = lax.dot_general(q, keys, (((1,), (1,)), ((), ())),
                                 preferred_element_type=jnp.float32)
             for c in range(tok_len // 128):
@@ -185,12 +201,12 @@
                     seen = seen & (lane + c * 128 <= row_tok + r // group_heads)
                 tiles.append(jnp.where(seen, tile, HIDDEN))
         top = functools.reduce(jnp.maximum, tiles)
-        top = jnp.max(top, axis=1, keepdims=True)
+        top = jnp.broadcast_to(jnp.max(top, axis=1, keepdims=True), (ROWS, 128))
         if state is not None:
             top = jnp.maximum(top, state[0])
         weights = [jnp.exp2((t - top) * scale) for t in tiles]
         total = functools.reduce(jnp.add, weights)
-        values = win[pl.ds(begin, CHUNK_BLOCKS), h, 1].reshape(width, head_dim)
+        values = win[pl.ds(begin, CHUNK_BLOCKS), 2 * h + 1].reshape(width, head_dim)
         packed = jnp.concatenate([w.astype(jnp.bfloat16) for w in weights], axis=1)
         product = jnp.dot(packed, values, preferred_element_type=jnp.float32)
         if state is None:
@@ -198,8 +214,20 @@
         rescale = jnp.exp2((state[0] - top) * scale)
         return top, state[1] * rescale + total, state[2] * rescale + product
 
-    def block(h, r):
+    def begin_rows(h, r):
         state = attend(h, r, chunks - 1, True, None)
+        at = pl.ds(r, ROWS)
+        top_scr[at, :] = state[0]
+        total_scr[at, :] = state[1]
+        sum_scr[at, :] = state[2]
+
+    def kept(r):
+        at = pl.ds(r, ROWS)
+        return top_scr[at, :], total_scr[at, :], sum_scr[at, :]
+
+    def block(h, r, state):
+        if state is None:
+            state = attend(h, r, chunks - 1, True, None)
         if chunks == 2:
             state = attend(h, r, 0, False, state)
         else:
@@ -213,7 +241,7 @@
     def rows_of(h, token0, dst, b):
         t = pl.multiple_of(token0 + b * toks, toks)
         r = pl.multiple_of(t * group_heads, ROWS)
-        dst(pl.multiple_of(b * toks, toks), block(h, r))
+        dst(pl.multiple_of(b * toks, toks), block(h, r, kept(r) if h == 0 else None))
 
     def store_sent(h, t, value):
         done[h, pl.ds(t, toks)] = value
@@ -226,32 +254,50 @@
             src_ref=done.at[h], dst_ref=out_ref.at[y, h], send_sem=out_send.at[h],
             recv_sem=out_recv.at[h], device_id={"head": 1 - y}, device_id_type=MESH)
 
+    for p in range(pieces):
+        pltpu.make_async_copy(kv_ref.at[p], win.at[own, p], local_sem.at[p]).wait()
+    early, late = stages(0)
+    for number, stage in enumerate(early):
+        stage()
+        if number == 1:
+            for p in range(2, pieces):
+                pump_own(p)
+
+    def spread(groups_of_stages, places):
+        per = -(-len(groups_of_stages) // places)
+        return [sum(groups_of_stages[c * per:(c + 1) * per], []) for c in range(places)]
+
+    def whole(h):
+        order = []
+        for s in range(1, depth + 1):
+            order += [both(pump_ring, s, h), both(pump_pair, s - 1, h)]
+        order += [both(pump_pair, depth, h)]
+        return order + [sum([both(pump_core, s, h) for s in range(depth + 1)], [])]
+
+    row_blocks = rows_total // ROWS
+    following = [[]] + spread(whole(1), 2 * row_blocks - 1)
+    for b, now in enumerate(spread(late, row_blocks)):
+        begin_rows(0, b * ROWS)
+        for stage in following[b] + now:
+            stage()
+
     for h in range(kv_heads):
-        pltpu.make_async_copy(kv_ref.at[h], win.at[own, h], local_sem.at[h]).wait()
-    for stage in stages(0):
-        stage()
-    for h in range(kv_heads):
-        pending = stages(h + 1) if h + 1 < kv_heads else []
-        per = -(-len(pending) // (2 * blocks_half))
+        if h == 0:
+            pending = following[row_blocks:]
+        elif h + 1 < kv_heads:
+            pending = spread(whole(h + 1), row_blocks)
+        else:
+            pending = [[]] * row_blocks
         for part, (token0, store) in enumerate(
                 (((1 - y) * half, store_sent), (y * half, store_own))):
-            if pending:
-                for b in range(blocks_half):
-                    rows_of(h, token0, functools.partial(store, h), b)
-                    for stage in pending[:per]:
-                        stage()
-                    pending = pending[per:]
-            else:
-                def step(b, _):
-                    rows_of(h, token0, functools.partial(store, h), b)
-                    return 0
-                lax.fori_loop(0, blocks_half, step, 0)
-            if part == 0:
-                out_copy(h).start()
-        for stage in pending:
-            stage()
-
-    for h in range(kv_heads):
+            for b in range(blocks_half):
+                rows_of(h, token0, functools.partial(store, h), b)
+                if part == 0 and b == blocks_half - 1:
+                    out_copy(h).start()
+                for stage in pending[part * blocks_half + b]:
+                    stage()
+
+    for h in range(pieces):
         send_ring(0, h, kv_ref.at[h], wait_sent)
         for s in range(depth + 1):
             src = win.at[slot(s, j), h]
@@ -261,6 +307,7 @@
             send_core(s, j, 0, h, src, wait_sent)
             m = j + 2 - 4 * x
             send_core(s, m, 1, h, win.at[slot(s, m), h], wait_sent)
+    for h in range(kv_heads):
         out_copy(h).wait()
 
 
@@ -272,10 +319,8 @@
     depth = -(-reach // MEMBERS)
     slots = MEMBERS * (depth + 1)
     kv = jnp.stack([key_rows, value_vectors]).transpose(2, 0, 1, 3)
-    i = lax.axis_index("ctx")
-    own_doc = lax.dynamic_slice_in_dim(doc_ids, i * tok_len, tok_len, 0)
-    begins = jnp.sum((doc_ids[None, :] < own_doc[:, None]).astype(jnp.int32), axis=1)
-    begins = jnp.broadcast_to(begins[:, None], (tok_len, 128))
+    pieces = 2 * kv_heads
+    kv = kv.reshape(pieces, tok_len, head_dim)
     half = tok_len // 2
     dma = pltpu.SemaphoreType.DMA
     out = pl.pallas_call(
@@ -285,20 +330,24 @@
         in_specs=[pl.BlockSpec(memory_space=pltpu.VMEM)] * 3,
         out_specs=pl.BlockSpec(memory_space=pltpu.VMEM),
         scratch_shapes=[
-            pltpu.VMEM((slots, kv_heads, 2, tok_len, head_dim), jnp.bfloat16),
+            pltpu.VMEM((slots, pieces, tok_len, head_dim), jnp.bfloat16),
             pltpu.VMEM((kv_heads, tok_len * group_heads, head_dim), jnp.bfloat16),
+            pltpu.VMEM((tok_len, 128), jnp.int32),
             pltpu.VMEM((tok_len * group_heads, 128), jnp.int32),
             pltpu.VMEM((kv_heads, half, group_heads, head_dim), jnp.bfloat16),
-            dma((depth, kv_heads)),
-            dma((depth + 1, kv_heads)),
-            dma((2, depth + 1, kv_heads)),
-            dma((slots, kv_heads)),
-            dma((kv_heads,)),
+            pltpu.VMEM((tok_len * group_heads, 128), jnp.float32),
+            pltpu.VMEM((tok_len * group_heads, 128), jnp.float32),
+            pltpu.VMEM((tok_len * group_heads, head_dim), jnp.float32),
+            dma((depth, pieces)),
+            dma((depth + 1, pieces)),
+            dma((2, depth + 1, pieces)),
+            dma((slots, pieces)),
+            dma((pieces,)),
             dma((kv_heads,)),
             dma((kv_heads,)),
         ],
         compiler_params=pltpu.CompilerParams(collective_id=0, has_side_effects=True),
-    )(queries, kv, begins)
+    )(queries, kv, doc_ids.reshape(-1, 128))
     return out.transpose(2, 0, 1, 3, 4).reshape(half, 2 * heads_here, head_dim)
 
 

time: 50 us -> 44.5 us (0.89)
  Pallas kernels: 42.5 us -> 39.7 us
  local copies, waits for them, and re-layouts: 4.89 us -> 3.11 us
  other arithmetic: 2 us -> 1.36 us
    pallas_call x1, Pallas kernels: 42.5 us -> 39.7 us  [body(): pl.pallas_call(functools.partial(kernel, n), out_shape=jax.ShapeDtypeStru...]
    reduce_sum x1 -> x0, other arithmetic: 1.28 us -> none  [body(): jnp.sum((doc_ids[None, :] < own_doc[:, None]).astype(jnp.int32), axis=1)]
    another operation x1 -> x0, local copies, waits for them, and re-layouts: 1 us -> none  [body(): kv = jnp.stack([key_rows, value_vectors]).transpose(2, 0, 1, 3)]
    dynamic_slice x1 -> x0, local copies, waits for them, and re-layouts: 0.76 us -> none  [body(): own_doc = lax.dynamic_slice_in_dim(doc_ids, i * tok_len, tok_len, 0)]
    broadcast_in_dim x1 -> x0, local copies, waits for them, and re-layouts: 0.76 us -> none  [body(): begins = jnp.broadcast_to(begins[:, None], (tok_len, 128))]
    transpose x0 -> x1, local copies, waits for them, and re-layouts: none -> 0.74 us  [body(): kv = jnp.stack([key_rows, value_vectors]).transpose(2, 0, 1, 3)]
    transpose x1, other arithmetic: 0.73 us -> 1.36 us  [body(): kv = jnp.stack([key_rows, value_vectors]).transpose(2, 0, 1, 3)]
where the time goes in v2:
time: 44.5 us; the launch traced here: 44.2 us
  Pallas kernels  39.7 us (89%)
  local copies, waits for them, and re-layouts  3.11 us (7%)
  other arithmetic  1.36 us (3%)
    pallas_call x1, Pallas kernels, body(): pl.pallas_call(functools.partial(kernel, n), out_shape=jax.ShapeDtypeStru...  39.7 us
    transpose x1, local copies, waits for them, and re-layouts, body(): return out.transpose(2, 0, 1, 3, 4).reshape(half, 2 * heads_here, head_dim)  2.37 us
    transpose x1, other arithmetic, body(): kv = jnp.stack([key_rows, value_vectors]).transpose(2, 0, 1, 3)  1.36 us

profile of v2, /device:TPU:16, one launch (start us, length us, event | category | flops | bytes accessed | tf_op | source)
XLA Modules:
  0.0 44.2 jit_solution(12716815738017540168)
XLA Ops:
  0.0 1.4 %maximum_bitcast_fusion = bf16[2,2,256,128]{3,0,2,1:T(2,128)(2,1)S(1)} fusion(bf16[1,256,2,128]{3,2,1,0:T(2,128)(2,1)} %bitcast.10, bf16[1,256,2,128]{3,2,1,0:T(2,128)(2,1)} %bitcast.11), kind=kLoop, calls=%fused_computation | loop fusion | flops 131072 | bytes 524288 | tf_op jit(solution)/shard_map/transpose | solution.py:321
  1.4 0.7 %copy.6 = bf16[2,2,256,128]{3,2,1,0:T(8,128)(2,1)} copy(bf16[2,2,256,128]{3,0,2,1:T(2,128)(2,1)S(1)} %maximum_bitcast_fusion) | data formatting | bytes 524288 | tf_op jit(solution)/shard_map/transpose | solution.py:321
  2.1 39.7 %shard_map.46 = bf16[2,2,128,8,128]{4,3,2,1,0:T(8,128)(2,1)} custom-call(bf16[256,16,128]{2,1,0:T(8,128)(2,1)} %q_ref.1, bf16[4,256,128]{2,1,0:T(8,128)(2,1)} %bitcast.9, s32[32,128]{1,0:T(8,128)} %bitcast.12), custom_call_target="tpu_custom_call" | custom-call | tf_op jit(solution)/shard_map/pallas_call | solution.py:326
  41.8 2.4 %copy.7 = bf16[128,2,2,8,128]{4,3,2,1,0:T(8,128)(2,1)} copy(bf16[128,2,2,8,128]{4,3,0,2,1:T(8,128)(2,1)} %bitcast.8) | data formatting | bytes 2097152 | tf_op jit(solution)/shard_map/transpose | solution.py:351

commit v3 on v2

--- a/solution.py
+++ b/solution.py
@@ -179,17 +179,16 @@
     lax.fori_loop(0, rows_total // ROWS, prepare, 0)
 
     chunks = (reach + 1) // CHUNK_BLOCKS
-    width = CHUNK_BLOCKS * tok_len
     lane = lax.broadcasted_iota(jnp.int32, (ROWS, 128), 1)
     row_tok = lax.broadcasted_iota(jnp.int32, (ROWS, 128), 0) // group_heads
 
-    def attend(h, r, chunk, newest, state):
+    def attend(h, r, low, count, newest, state):
         q = q_scr[h, pl.ds(r, ROWS), :]
-        begin = first + chunk * CHUNK_BLOCKS
-        key_base = (i - reach + chunk * CHUNK_BLOCKS) * tok_len
+        begin = first + low
+        key_base = (i - reach + low) * tok_len
         st = start_scr[pl.ds(r, ROWS), :] - key_base - lane
         tiles = []
-        for b in range(CHUNK_BLOCKS):
+        for b in range(count):
             keys = win[begin + b, 2 * h]
             s = lax.dot_general(q, keys, (((1,), (1,)), ((), ())),
                                 preferred_element_type=jnp.float32)
@@ -197,7 +196,7 @@
                 off = b * tok_len + c * 128
                 tile = s[:, c * 128:(c + 1) * 128]
                 seen = st <= off
-                if newest and b == CHUNK_BLOCKS - 1:
+                if newest and b == count - 1:
                     seen = seen & (lane + c * 128 <= row_tok + r // group_heads)
                 tiles.append(jnp.where(seen, tile, HIDDEN))
         top = functools.reduce(jnp.maximum, tiles)
@@ -206,7 +205,7 @@
             top = jnp.maximum(top, state[0])
         weights = [jnp.exp2((t - top) * scale) for t in tiles]
         total = functools.reduce(jnp.add, weights)
-        values = win[pl.ds(begin, CHUNK_BLOCKS), 2 * h + 1].reshape(width, head_dim)
+        values = win[pl.ds(begin, count), 2 * h + 1].reshape(count * tok_len, head_dim)
         packed = jnp.concatenate([w.astype(jnp.bfloat16) for w in weights], axis=1)
         product = jnp.dot(packed, values, preferred_element_type=jnp.float32)
         if state is None:
@@ -214,25 +213,35 @@
         rescale = jnp.exp2((state[0] - top) * scale)
         return top, state[1] * rescale + total, state[2] * rescale + product
 
-    def begin_rows(h, r):
-        state = attend(h, r, chunks - 1, True, None)
+    def keep(h, r, state):
         at = pl.ds(r, ROWS)
-        top_scr[at, :] = state[0]
-        total_scr[at, :] = state[1]
-        sum_scr[at, :] = state[2]
-
-    def kept(r):
+        top_scr[h, at, :] = state[0]
+        total_scr[h, at, :] = state[1]
+        sum_scr[h, at, :] = state[2]
+
+    def kept(h, r):
         at = pl.ds(r, ROWS)
-        return top_scr[at, :], total_scr[at, :], sum_scr[at, :]
-
-    def block(h, r, state):
-        if state is None:
-            state = attend(h, r, chunks - 1, True, None)
+        return top_scr[h, at, :], total_scr[h, at, :], sum_scr[h, at, :]
+
+    def recent(h, r):
+        low = reach + 1 - CHUNK_BLOCKS
+        return attend(h, r, low, CHUNK_BLOCKS - 1, False, kept(h, r))
+
+    def own_rows(h):
+        def step(b, _):
+            r = pl.multiple_of(b * ROWS, ROWS)
+            keep(h, r, attend(h, r, reach, 1, True, None))
+            return 0
+        lax.fori_loop(0, rows_total // ROWS, step, 0)
+
+    def block(h, r):
+        state = kept(h, r) if h == 0 else recent(h, r)
         if chunks == 2:
-            state = attend(h, r, 0, False, state)
+            state = attend(h, r, 0, CHUNK_BLOCKS, False, state)
         else:
             state = lax.fori_loop(
-                1, chunks, lambda c, st: attend(h, r, chunks - 1 - c, False, st), state)
+                1, chunks, lambda c, st: attend(
+                    h, r, (chunks - 1 - c) * CHUNK_BLOCKS, CHUNK_BLOCKS, False, st), state)
         total = jnp.sum(state[1], axis=1, keepdims=True)
         return (state[2] / total).reshape(toks, group_heads, head_dim).astype(jnp.bfloat16)
 
@@ -241,7 +250,7 @@
     def rows_of(h, token0, dst, b):
         t = pl.multiple_of(token0 + b * toks, toks)
         r = pl.multiple_of(t * group_heads, ROWS)
-        dst(pl.multiple_of(b * toks, toks), block(h, r, kept(r) if h == 0 else None))
+        dst(pl.multiple_of(b * toks, toks), block(h, r))
 
     def store_sent(h, t, value):
         done[h, pl.ds(t, toks)] = value
@@ -256,12 +265,15 @@
 
     for p in range(pieces):
         pltpu.make_async_copy(kv_ref.at[p], win.at[own, p], local_sem.at[p]).wait()
+    own_rows(0)
     early, late = stages(0)
     for number, stage in enumerate(early):
         stage()
         if number == 1:
             for p in range(2, pieces):
                 pump_own(p)
+            for h in range(1, kv_heads):
+                own_rows(h)
 
     def spread(groups_of_stages, places):
         per = -(-len(groups_of_stages) // places)
@@ -277,7 +289,7 @@
     row_blocks = rows_total // ROWS
     following = [[]] + spread(whole(1), 2 * row_blocks - 1)
     for b, now in enumerate(spread(late, row_blocks)):
-        begin_rows(0, b * ROWS)
+        keep(0, b * ROWS, recent(0, b * ROWS))
         for stage in following[b] + now:
             stage()
 
@@ -335,9 +347,9 @@
             pltpu.VMEM((tok_len, 128), jnp.int32),
             pltpu.VMEM((tok_len * group_heads, 128), jnp.int32),
             pltpu.VMEM((kv_heads, half, group_heads, head_dim), jnp.bfloat16),
-            pltpu.VMEM((tok_len * group_heads, 128), jnp.float32),
-            pltpu.VMEM((tok_len * group_heads, 128), jnp.float32),
-            pltpu.VMEM((tok_len * group_heads, head_dim), jnp.float32),
+            pltpu.VMEM((kv_heads, tok_len * group_heads, 128), jnp.float32),
+            pltpu.VMEM((kv_heads, tok_len * group_heads, 128), jnp.float32),
+            pltpu.VMEM((kv_heads, tok_len * group_heads, head_dim), jnp.float32),
             dma((depth, pieces)),
             dma((depth + 1, pieces)),
             dma((2, depth + 1, pieces)),

time: 44.5 us -> 43.5 us (0.978)
  Pallas kernels: 39.7 us -> 38.9 us
    pallas_call x1, Pallas kernels: 39.7 us -> 38.9 us  [body(): pl.pallas_call(functools.partial(kernel, n), out_shape=jax.ShapeDtypeStru...]
where the time goes in v3:
time: 43.5 us; the launch traced here: 43.4 us
  Pallas kernels  38.9 us (89%)
  local copies, waits for them, and re-layouts  3.11 us (7%)
  other arithmetic  1.36 us (3%)
    pallas_call x1, Pallas kernels, body(): pl.pallas_call(functools.partial(kernel, n), out_shape=jax.ShapeDtypeStru...  38.9 us
    transpose x1, local copies, waits for them, and re-layouts, body(): return out.transpose(2, 0, 1, 3, 4).reshape(half, 2 * heads_here, head_dim)  2.37 us
    transpose x1, other arithmetic, body(): kv = jnp.stack([key_rows, value_vectors]).transpose(2, 0, 1, 3)  1.36 us

profile of v3, /device:TPU:16, one launch (start us, length us, event | category | flops | bytes accessed | tf_op | source)
XLA Modules:
  0.0 43.4 jit_solution(3582790113559286053)
XLA Ops:
  0.0 1.4 %maximum_bitcast_fusion = bf16[2,2,256,128]{3,0,2,1:T(2,128)(2,1)S(1)} fusion(bf16[1,256,2,128]{3,2,1,0:T(2,128)(2,1)} %bitcast.10, bf16[1,256,2,128]{3,2,1,0:T(2,128)(2,1)} %bitcast.11), kind=kLoop, calls=%fused_computation | loop fusion | flops 131072 | bytes 524288 | tf_op jit(solution)/shard_map/transpose | solution.py:333
  1.4 0.7 %copy.6 = bf16[2,2,256,128]{3,2,1,0:T(8,128)(2,1)} copy(bf16[2,2,256,128]{3,0,2,1:T(2,128)(2,1)S(1)} %maximum_bitcast_fusion) | data formatting | bytes 524288 | tf_op jit(solution)/shard_map/transpose | solution.py:333
  2.1 38.9 %shard_map.46 = bf16[2,2,128,8,128]{4,3,2,1,0:T(8,128)(2,1)} custom-call(bf16[256,16,128]{2,1,0:T(8,128)(2,1)} %q_ref.1, bf16[4,256,128]{2,1,0:T(8,128)(2,1)} %bitcast.9, s32[32,128]{1,0:T(8,128)} %bitcast.12), custom_call_target="tpu_custom_call" | custom-call | tf_op jit(solution)/shard_map/pallas_call | solution.py:338
  41.0 2.4 %copy.7 = bf16[128,2,2,8,128]{4,3,2,1,0:T(8,128)(2,1)} copy(bf16[128,2,2,8,128]{4,3,0,2,1:T(8,128)(2,1)} %bitcast.8) | data formatting | bytes 2097152 | tf_op jit(solution)/shard_map/transpose | solution.py:363

commit v4 on v3

--- a/solution.py
+++ b/solution.py
@@ -272,6 +272,7 @@
         if number == 1:
             for p in range(2, pieces):
                 pump_own(p)
+        if number == 3:
             for h in range(1, kv_heads):
                 own_rows(h)
 

time: 43.5 us -> 43.5 us (level)
  no operation moved by 1% of the time
where the time goes in v4:
time: 43.5 us; the launch traced here: 43.4 us
  Pallas kernels  38.9 us (89%)
  local copies, waits for them, and re-layouts  3.11 us (7%)
  other arithmetic  1.36 us (3%)
    pallas_call x1, Pallas kernels, body(): pl.pallas_call(functools.partial(kernel, n), out_shape=jax.ShapeDtypeStru...  38.9 us
    transpose x1, local copies, waits for them, and re-layouts, body(): return out.transpose(2, 0, 1, 3, 4).reshape(half, 2 * heads_here, head_dim)  2.37 us
    transpose x1, other arithmetic, body(): kv = jnp.stack([key_rows, value_vectors]).transpose(2, 0, 1, 3)  1.36 us

profile of v4, /device:TPU:16, one launch (start us, length us, event | category | flops | bytes accessed | tf_op | source)
XLA Modules:
  0.0 43.4 jit_solution(12953580039983149546)
XLA Ops:
  0.0 1.4 %maximum_bitcast_fusion = bf16[2,2,256,128]{3,0,2,1:T(2,128)(2,1)S(1)} fusion(bf16[1,256,2,128]{3,2,1,0:T(2,128)(2,1)} %bitcast.10, bf16[1,256,2,128]{3,2,1,0:T(2,128)(2,1)} %bitcast.11), kind=kLoop, calls=%fused_computation | loop fusion | flops 131072 | bytes 524288 | tf_op jit(solution)/shard_map/transpose | solution.py:334
  1.4 0.7 %copy.6 = bf16[2,2,256,128]{3,2,1,0:T(8,128)(2,1)} copy(bf16[2,2,256,128]{3,0,2,1:T(2,128)(2,1)S(1)} %maximum_bitcast_fusion) | data formatting | bytes 524288 | tf_op jit(solution)/shard_map/transpose | solution.py:334
  2.1 38.9 %shard_map.46 = bf16[2,2,128,8,128]{4,3,2,1,0:T(8,128)(2,1)} custom-call(bf16[256,16,128]{2,1,0:T(8,128)(2,1)} %q_ref.1, bf16[4,256,128]{2,1,0:T(8,128)(2,1)} %bitcast.9, s32[32,128]{1,0:T(8,128)} %bitcast.12), custom_call_target="tpu_custom_call" | custom-call | tf_op jit(solution)/shard_map/pallas_call | solution.py:339
  41.0 2.4 %copy.7 = bf16[128,2,2,8,128]{4,3,2,1,0:T(8,128)(2,1)} copy(bf16[128,2,2,8,128]{4,3,0,2,1:T(8,128)(2,1)} %bitcast.8) | data formatting | bytes 2097152 | tf_op jit(solution)/shard_map/transpose | solution.py:364
